TPU v7x, 512 devices: a whole 4x8x8 slice. The times are simulated.
512 devices in a mesh: row: 32 (over z_hi, x, core), col: 16 (over y, z_lo).
Axes of the slice: x: 4, y: 8, z: 8 (z_hi: 4, z_lo: 2; z = z_hi * 2 + z_lo), core: 2. Of those that a mesh axis runs over, the one named last changes fastest.
Arguments:
- source_points: float32 [3, 131072], P(None, 'col'), may hold values from 0 to 1
- source_areas: float32 [131072], P('col'), may hold values from 0.02 to 0.2
- source_fill: int32 [512], P('col'), may hold values from 128 to 256
- target_points: float32 [3, 131072], P(None, 'row'), may hold values from 0 to 1
- target_fill: int32 [512], P('row'), may hold values from 128 to 256
- charges: bfloat16 [64, 131072], P('row', 'col'), may hold values from -6 to 6
- near_fill: int32 [32, 16], P('row', 'col'), may hold values from 32 to 256, as said below
- near_source: int32 [32, 4096], P('row', 'col'), may hold values from 0 to 31
- near_target: int32 [32, 4096], P('row', 'col'), may hold values from 0 to 15
- far_source: int32 [32, 1536], P('row', 'col'), may hold values from 0 to 31
- far_target: int32 [32, 1536], P('row', 'col'), may hold values from 0 to 15
- far_rank: int32 [32, 1536], P('row', 'col'), may hold values from 8 to 32
- left_basis: bfloat16 [32, 1536, 32, 256], P('row', 'col'), may hold values from -0.25 to 0.25
- right_basis: bfloat16 [32, 1536, 32, 256], P('row', 'col'), may hold values from -0.375 to 0.375
Outputs:
- potential: float32 [64, 131072], P('col', 'row')
Inputs may be any that keep to these rules, and one draw needn't show every extreme that they name: `near_fill`: used slots are the first ones of a device; in every row some device uses all 256. `near_source`: index among the 32 source leaves of the device's column group. `near_target`: index among the 16 target leaves of the device's row group. `far_source`: index among the 32 source leaves of the device's column group. `far_target`: index among the 16 target leaves of the device's row group. `far_rank`: factor rows from the rank on are padding.
All inputs are finite; a program needn't handle non-finite values.
Results may differ from a plain program's by a relative error of at most 0.0029.
Values may be sent and summed in bfloat16 or wider, within the bound.
A program may use at most 64 MiB of HBM per device.

v0:
```python
import jax
import jax.numpy as jnp
from jax import lax
from jax.experimental import pallas as pl
from jax.experimental.pallas import tpu as pltpu
from jax.sharding import PartitionSpec as P

INV_FOUR_PI = 0.07957747154594767
SOFTENING_SQ = 0.0025
MESH = pl.DeviceIdType.MESH

LEAF = 256
RANK = 32
RL = 16
CL = 32
NEAR = 256
FAR = 96
N_ROW = 32
N_COL = 16
RHS = 64
NS = CL * LEAF
NT = RL * LEAF
FEAT = 48
ZERO = RL
FAR_BASE = RL + NEAR - FAR
SUMS = RL + NEAR

ENTRY_UNROLL = 16
FAR_UNROLL = 8
NEAR_UNROLL = 16
LANES = 128
F32 = jnp.float32
BF16 = jnp.bfloat16


def split3(value):
    high = value.astype(BF16).astype(F32)
    rest = value - high
    middle = rest.astype(BF16).astype(F32)
    low = (rest - middle).astype(BF16).astype(F32)
    return high, middle, low


def kernel(
    near_prev,
    near_last,
    far_prev,
    far_last,
    near_source,
    near_target,
    far_source,
    far_rank,
    source_fill,
    target_fill,
    source_points,
    source_areas,
    target_points,
    charges,
    left_hbm,
    right_hbm,
    out,
    grid_raw,
    grid,
    entries,
    sums,
    source_feat,
    target_feat,
    scaled,
    weight,
    plain,
    left,
    right,
    outgoing,
    from_side,
    merged,
    from_along,
    own_sem,
    basis_sem,
    z_send,
    z_recv,
    x_send,
    x_recv,
    pair_send,
    pair_recv,
    side_send,
    side_recv,
    along_send,
    along_recv,
):
    row = lax.axis_index("row")
    col = lax.axis_index("col")
    core = lax.rem(row, 2)
    x = lax.rem(row // 2, 4)
    z = row // 8

    def row_of(zz, xx, kk):
        return (zz * 4 + xx) * 2 + kk

    def back(a, d):
        return lax.rem(a + 4 - d, 4)

    def ahead(a, d):
        return lax.rem(a + d, 4)

    own_copy = pltpu.make_async_copy(charges, grid_raw.at[row], own_sem)
    own_copy.start()
    left_copy = pltpu.make_async_copy(left_hbm.at[0], left, basis_sem.at[0])
    right_copy = pltpu.make_async_copy(right_hbm.at[0], right, basis_sem.at[1])
    left_copy.start()
    right_copy.start()

    barrier = pltpu.get_barrier_semaphore()
    partner = row_of(z, x, 1 - core)
    peers = [partner]
    peers += [row_of(ahead(z, d), x, core) for d in (1, 2, 3)]
    peers += [row_of(z, ahead(x, d), core) for d in (1, 2, 3)]
    for peer in peers:
        pl.semaphore_signal(barrier, inc=1, device_id=(peer, col), device_id_type=MESH)
    for d in range(1, N_COL):
        pl.semaphore_signal(
            barrier, inc=1, device_id=(row, lax.rem(col + d, N_COL)), device_id_type=MESH
        )
    pl.semaphore_wait(barrier, len(peers) + N_COL - 1)

    def send(source, slot, peer, send_sem, recv_sem):
        return pltpu.make_async_remote_copy(
            src_ref=source,
            dst_ref=grid_raw.at[slot],
            send_sem=send_sem,
            recv_sem=recv_sem,
            device_id=(peer, col),
            device_id_type=MESH,
        )

    def z_copy(dz):
        return send(
            charges, row, row_of(ahead(z, dz), x, core), z_send.at[dz - 1], z_recv.at[dz - 1]
        )

    def x_copy(dx, dz):
        slot = row_of(back(z, dz), x, core)
        source = charges if dz == 0 else grid_raw.at[slot]
        return send(
            source,
            slot,
            row_of(z, ahead(x, dx), core),
            x_send.at[dx - 1, dz],
            x_recv.at[dx - 1, dz],
        )

    def pair_copy(dz, dx):
        slot = row_of(back(z, dz), back(x, dx), core)
        source = charges if dz == 0 and dx == 0 else grid_raw.at[slot]
        return send(source, slot, partner, pair_send.at[dz, dx], pair_recv.at[dz, dx])

    started = []

    def go(copy):
        copy.start()
        started.append(copy)

    for dz in (2, 1, 3):
        go(z_copy(dz))
    for dx in (2, 1, 3):
        go(x_copy(dx, 0))
    go(pair_copy(0, 0))

    centred = source_points[...] - 0.5
    area = source_areas[...].reshape(1, NS) * INV_FOUR_PI
    weight[...] = 1.0 / (area * area)
    plain[0:3, :] = centred * -2.0
    plain[3:4, :] = jnp.ones((1, NS), F32)
    squares = centred * centred
    plain[4:5, :] = squares[0:1] + squares[1:2] + squares[2:3] + SOFTENING_SQ
    plain[5:8, :] = jnp.zeros((3, NS), F32)

    def source_leaf(s, carry):
        points = pl.ds(pl.multiple_of(s * LEAF, LEAF), LEAF)
        high, middle, low = split3(plain[:, points] * weight[:, points])
        stacked = jnp.concatenate([high, high, middle, middle, high, low], 0)
        source_feat[s] = stacked.T.astype(BF16)
        return carry

    lax.fori_loop(0, CL, source_leaf, 0)

    away = target_points[...] - 0.5
    scaled[0:3, :] = away
    squares = away * away
    scaled[3:4, :] = squares[0:1] + squares[1:2] + squares[2:3]
    scaled[4:5, :] = jnp.ones((1, NT), F32)
    scaled[5:8, :] = jnp.zeros((3, NT), F32)

    def target_leaf(t, carry):
        points = pl.ds(pl.multiple_of(t * LEAF, LEAF), LEAF)
        high, middle, low = split3(scaled[:, points])
        stacked = jnp.concatenate([high, middle, high, middle, low, high], 0)
        target_feat[t] = stacked.astype(BF16)
        return carry

    lax.fori_loop(0, RL, target_leaf, 0)

    def entry_step(step, carry):
        for u in range(ENTRY_UNROLL):
            k = step * ENTRY_UNROLL + u
            scaled_sq = jnp.dot(
                source_feat[near_source[0, k]],
                target_feat[near_target[0, k]],
                preferred_element_type=F32,
            )
            entries[k] = lax.rsqrt(scaled_sq).astype(BF16)
        return carry

    def some_entries(first, last):
        lax.fori_loop(first // ENTRY_UNROLL, last // ENTRY_UNROLL, entry_step, 0)

    def from_z(dz):
        z_copy(dz).wait_recv()
        for dx in (2, 1, 3):
            go(x_copy(dx, dz))
        go(pair_copy(dz, 0))

    def from_x(dx, dz):
        x_copy(dx, dz).wait_recv()
        go(pair_copy(dz, dx))

    some_entries(0, 48)
    from_z(1)
    from_z(3)
    some_entries(48, 80)
    from_z(2)
    for dx in (1, 3, 2):
        from_x(dx, 0)
    some_entries(80, 144)
    for dz in (1, 3):
        for dx in (1, 3, 2):
            from_x(dx, dz)
    some_entries(144, 224)
    for dx in (1, 3, 2):
        from_x(dx, 2)
    some_entries(224, NEAR)
    own_copy.wait()
    for dz in range(4):
        for dx in range(4):
            pair_copy(dz, dx).wait_recv()
    for copy in started:
        copy.wait_send()

    lane = lax.broadcasted_iota(jnp.int32, (RHS, LEAF), 1)

    def charge_leaf(s, carry):
        points = pl.ds(pl.multiple_of(s * LEAF, LEAF), LEAF)
        block = grid_raw[:, :, points].reshape(RHS, LEAF)
        grid[s] = jnp.where(lane < source_fill[s], block.astype(F32), 0.0).astype(BF16)
        return carry

    lax.fori_loop(0, CL, charge_leaf, 0)

    left_copy.wait()
    right_copy.wait()
    sums[ZERO] = jnp.zeros((RHS, LEAF), F32)
    rank_lane = lax.broadcasted_iota(jnp.int32, (RHS, RANK), 1)

    def far_step(step, carry):
        blocks = []
        for u in range(FAR_UNROLL):
            k = step * FAR_UNROLL + u
            coefficients = lax.dot_general(
                grid[far_source[0, k]],
                right[k],
                (((1,), (1,)), ((), ())),
                preferred_element_type=F32,
            )
            coefficients = jnp.where(rank_lane < far_rank[0, k], coefficients, 0.0)
            blocks.append(
                jnp.dot(coefficients.astype(BF16), left[k], preferred_element_type=F32)
            )
        for u in range(FAR_UNROLL):
            k = step * FAR_UNROLL + u
            sums[FAR_BASE + k] = blocks[u] + sums[far_prev[0, k]]
        return carry

    lax.fori_loop(0, FAR // FAR_UNROLL, far_step, 0)

    for t in range(RL):
        sums[t] = sums[far_last[0, t]]

    def near_step(step, carry):
        blocks = []
        for u in range(NEAR_UNROLL):
            k = step * NEAR_UNROLL + u
            blocks.append(
                jnp.dot(grid[near_source[0, k]], entries[k], preferred_element_type=F32)
            )
        for u in range(NEAR_UNROLL):
            k = step * NEAR_UNROLL + u
            sums[RL + k] = blocks[u] + sums[near_prev[0, k]]
        return carry

    lax.fori_loop(0, NEAR // NEAR_UNROLL, near_step, 0)

    def pack_target(t, carry):
        points = pl.ds(pl.multiple_of(t * LEAF, LEAF), LEAF)
        value = jnp.where(lane < target_fill[t], sums[near_last[0, t]], 0.0).astype(BF16)
        for c in range(N_COL):
            outgoing[c, :, points] = value[4 * c : 4 * c + 4]
        return carry

    lax.fori_loop(0, RL, pack_target, 0)

    along = col // 2
    side = lax.rem(col, 2)

    def owner(d, which):
        return lax.rem(along + d, 8) * 2 + which

    def side_copy(d):
        return pltpu.make_async_remote_copy(
            src_ref=outgoing.at[owner(d, 1 - side)],
            dst_ref=from_side.at[d],
            send_sem=side_send.at[d],
            recv_sem=side_recv.at[d],
            device_id=(row, owner(0, 1 - side)),
            device_id_type=MESH,
        )

    def along_copy(d):
        return pltpu.make_async_remote_copy(
            src_ref=merged.at[d],
            dst_ref=from_along.at[d - 1],
            send_sem=along_send.at[d - 1],
            recv_sem=along_recv.at[d - 1],
            device_id=(row, owner(d, side)),
            device_id_type=MESH,
        )

    order = (4, 3, 5, 2, 6, 1, 7)
    for d in order + (0,):
        side_copy(d).start()
    for d in order:
        side_copy(d).wait_recv()
        both = outgoing[owner(d, side)].astype(F32) + from_side[d].astype(F32)
        merged[d] = both.astype(BF16)
        along_copy(d).start()
    side_copy(0).wait_recv()
    for d in order:
        along_copy(d).wait_recv()

    def add_up(step, carry):
        points = pl.ds(pl.multiple_of(step * 512, 512), 512)
        total = outgoing[col, :, points].astype(F32) + from_side[0, :, points].astype(F32)
        for d in order:
            total = total + from_along[d - 1, :, points].astype(F32)
        out[:, points] = total
        return carry

    lax.fori_loop(0, NT // 512, add_up, 0)
    for d in order:
        along_copy(d).wait_send()
        side_copy(d).wait_send()
    side_copy(0).wait_send()


def chain_kernel(near_target, far_target, near_fill, near_prev, near_last, far_prev, far_last):
    def chains(target, count, place, empty):
        across = jnp.broadcast_to(target, (count, count))
        down = across.T
        at_down = lax.broadcasted_iota(jnp.int32, (count, count), 0)
        at_across = lax.broadcasted_iota(jnp.int32, (count, count), 1)
        hit = (across == down) & (at_down < at_across)
        prev = jnp.max(jnp.where(hit, at_down + place, -1), axis=0, keepdims=True)
        return jnp.maximum(prev, empty), down

    def latest(down, count, place, live, empty):
        slot = lax.broadcasted_iota(jnp.int32, (count, LANES), 0)
        leaf = lax.broadcasted_iota(jnp.int32, (count, LANES), 1)
        hit = (down[:, :LANES] == leaf) & (slot < live)
        last = jnp.max(jnp.where(hit, slot + place, -1), axis=0, keepdims=True)
        return jnp.maximum(last, empty)

    leaf = lax.broadcasted_iota(jnp.int32, (1, LANES), 1)
    prev, down = chains(near_target[...], NEAR, RL, near_target[...])
    near_prev[...] = prev
    near_last[...] = latest(down, NEAR, RL, near_fill[0, 0], jnp.minimum(leaf, RL - 1))
    far = jnp.concatenate([far_target[...], jnp.full((1, LANES - FAR), RL, jnp.int32)], 1)
    prev, down = chains(far, LANES, FAR_BASE, ZERO)
    far_prev[...] = prev
    far_last[...] = latest(down, LANES, FAR_BASE, FAR, ZERO)


def shards(
    source_points,
    source_areas,
    source_fill,
    target_points,
    target_fill,
    charges,
    near_fill,
    near_source,
    near_target,
    far_source,
    far_target,
    far_rank,
    left_basis,
    right_basis,
):
    smem = pl.BlockSpec(memory_space=pltpu.SMEM)
    vmem = pl.BlockSpec(memory_space=pltpu.VMEM)
    hbm = pl.BlockSpec(memory_space=pl.ANY)
    dma = pltpu.SemaphoreType.DMA
    chains = pl.pallas_call(
        chain_kernel,
        name="chains",
        out_shape=[
            jax.ShapeDtypeStruct((1, NEAR), jnp.int32),
            jax.ShapeDtypeStruct((1, LANES), jnp.int32),
            jax.ShapeDtypeStruct((1, LANES), jnp.int32),
            jax.ShapeDtypeStruct((1, LANES), jnp.int32),
        ],
        in_specs=[vmem, vmem, smem],
        out_specs=[vmem] * 4,
    )(near_target, far_target, near_fill)
    return pl.pallas_call(
        kernel,
        name="block_low_rank",
        out_shape=jax.ShapeDtypeStruct((RHS // N_COL, NT), F32),
        in_specs=[smem] * 10 + [vmem] * 4 + [hbm] * 2,
        out_specs=vmem,
        scratch_shapes=[
            pltpu.VMEM((N_ROW, RHS // N_ROW, NS), BF16),
            pltpu.VMEM((CL, RHS, LEAF), BF16),
            pltpu.VMEM((NEAR, LEAF, LEAF), BF16),
            pltpu.VMEM((SUMS, RHS, LEAF), F32),
            pltpu.VMEM((CL, LEAF, FEAT), BF16),
            pltpu.VMEM((RL, FEAT, LEAF), BF16),
            pltpu.VMEM((8, NT), F32),
            pltpu.VMEM((1, NS), F32),
            pltpu.VMEM((8, NS), F32),
            pltpu.VMEM((FAR, RANK, LEAF), BF16),
            pltpu.VMEM((FAR, RANK, LEAF), BF16),
            pltpu.VMEM((N_COL, RHS // N_COL, NT), BF16),
            pltpu.VMEM((8, RHS // N_COL, NT), BF16),
            pltpu.VMEM((8, RHS // N_COL, NT), BF16),
            pltpu.VMEM((7, RHS // N_COL, NT), BF16),
            dma(()),
            dma((2,)),
            dma((3,)),
            dma((3,)),
            dma((3, 4)),
            dma((3, 4)),
            dma((4, 4)),
            dma((4, 4)),
            dma((8,)),
            dma((8,)),
            dma((7,)),
            dma((7,)),
        ],
        compiler_params=pltpu.CompilerParams(
            collective_id=0, has_side_effects=True, vmem_limit_bytes=64 * 1024 * 1024 - 65536
        ),
    )(
        *chains,
        near_source,
        near_target,
        far_source,
        far_rank,
        source_fill,
        target_fill,
        source_points,
        source_areas,
        target_points,
        charges,
        left_basis,
        right_basis,
    )


def solution(mesh):
    placed = (
        P(None, "col"),
        P("col"),
        P("col"),
        P(None, "row"),
        P("row"),
        P("row", "col"),
        P("row", "col"),
        P("row", "col"),
        P("row", "col"),
        P("row", "col"),
        P("row", "col"),
        P("row", "col"),
        P("row", "col", None, None),
        P("row", "col", None, None),
    )
    return jax.shard_map(
        shards, mesh=mesh, in_specs=placed, out_specs=P("col", "row"), check_vma=False
    )
```

profile of v0, /device:TPU:1, one launch (start us, length us, event | category | flops | bytes accessed | tf_op | source)
XLA Modules:
  0.0 59.6 jit_solution(9571274298202223035)
XLA Ops:
  0.7 1.4 %chains.1 = (s32[1,256]{1,0:T(1,128)}, s32[1,128]{1,0:T(1,128)}, s32[1,128]{1,0:T(1,128)}, s32[1,128]{1,0:T(1,128)}) custom-call(s32[1,256]{1,0:T(1,128)} %near_target.3, s32[1,96]{1,0:T(1,128)} %far_target.1, s32[1,1]{1,0:T(1,128)S(6)} %copy.16.near_fill), custom_call_target="tpu_custom_call" | custom-call | tf_op jit(solution)/shard_map/chains/pallas_call | solution.py:410
  2.1 56.0 %block_low_rank.1 = f32[4,4096]{1,0:T(4,128)} custom-call(s32[1,256]{1,0:T(1,128)} %get-tuple-element.9.near_prev, s32[1,128]{1,0:T(1,128)} %get-tuple-element.10.near_last, s32[1,128]{1,0:T(1,128)} %get-tuple-element.11.far_prev, s32[1,128]{1,0:T(1,128)} %get-tuple-element.12.far_last, s32[1,256]{1,0:T(1,128)} %near_source.1, s32[1,256]{1,0:T(1,128)} %near_target.3, ...), custom_call_target="tpu_custom_call" | custom-call | tf_op jit(solution)/shard_map/block_low_rank/pallas_call | solution.py:422
  58.1 1.5 %copy.17 = f32[4,4096]{1,0:T(4,128)} copy(f32[4,4096]{1,0:T(4,128)} %block_low_rank.1) | data formatting | bytes 131072
where the time goes:
time: 59.8 us; the launch traced here: 59.6 us
  Pallas kernels  57.4 us (96%)
  local copies, waits for them, and re-layouts  1.47 us (2%)
  between operations  0.66 us (1%)
    pallas_call x1, Pallas kernels, shards(): pl.pallas_call(kernel, name='block_low_rank', out_shape=jax.ShapeDtypeStr...  56 us
    unnamed x1, local copies, waits for them, and re-layouts  1.47 us
    pallas_call x1, Pallas kernels, shards(): pl.pallas_call(chain_kernel, name='chains', out_shape=[jax.ShapeDtypeStru...  1.43 us

commit v1 on v0

--- a/solution.py
+++ b/solution.py
@@ -25,9 +25,9 @@
 FAR_BASE = RL + NEAR - FAR
 SUMS = RL + NEAR
 
-ENTRY_UNROLL = 16
-FAR_UNROLL = 8
-NEAR_UNROLL = 16
+ENTRY_UNROLL = 32
+FAR_UNROLL = 16
+NEAR_UNROLL = 32
 LANES = 128
 F32 = jnp.float32
 BF16 = jnp.bfloat16
@@ -70,7 +70,9 @@
     plain,
     left,
     right,
+    coefficients,
     outgoing,
+    kept,
     from_side,
     merged,
     from_along,
@@ -120,6 +122,40 @@
         pl.semaphore_signal(
             barrier, inc=1, device_id=(row, lax.rem(col + d, N_COL)), device_id_type=MESH
         )
+    centred = source_points[...] - 0.5
+    area = source_areas[...].reshape(1, NS) * INV_FOUR_PI
+    weight[...] = 1.0 / (area * area)
+    plain[0:3, :] = centred * -2.0
+    plain[3:4, :] = jnp.ones((1, NS), F32)
+    squares = centred * centred
+    plain[4:5, :] = squares[0:1] + squares[1:2] + squares[2:3] + SOFTENING_SQ
+    plain[5:8, :] = jnp.zeros((3, NS), F32)
+
+    def source_leaf(s, carry):
+        points = pl.ds(pl.multiple_of(s * LEAF, LEAF), LEAF)
+        high, middle, low = split3(plain[:, points] * weight[:, points])
+        stacked = jnp.concatenate([high, high, middle, middle, high, low], 0)
+        source_feat[s] = stacked.T.astype(BF16)
+        return carry
+
+    lax.fori_loop(0, CL, source_leaf, 0)
+
+    away = target_points[...] - 0.5
+    scaled[0:3, :] = away
+    squares = away * away
+    scaled[3:4, :] = squares[0:1] + squares[1:2] + squares[2:3]
+    scaled[4:5, :] = jnp.ones((1, NT), F32)
+    scaled[5:8, :] = jnp.zeros((3, NT), F32)
+
+    def target_leaf(t, carry):
+        points = pl.ds(pl.multiple_of(t * LEAF, LEAF), LEAF)
+        high, middle, low = split3(scaled[:, points])
+        stacked = jnp.concatenate([high, middle, high, middle, low, high], 0)
+        target_feat[t] = stacked.astype(BF16)
+        return carry
+
+    lax.fori_loop(0, RL, target_leaf, 0)
+
     pl.semaphore_wait(barrier, len(peers) + N_COL - 1)
 
     def send(source, slot, peer, send_sem, recv_sem):
@@ -165,40 +201,6 @@
         go(x_copy(dx, 0))
     go(pair_copy(0, 0))
 
-    centred = source_points[...] - 0.5
-    area = source_areas[...].reshape(1, NS) * INV_FOUR_PI
-    weight[...] = 1.0 / (area * area)
-    plain[0:3, :] = centred * -2.0
-    plain[3:4, :] = jnp.ones((1, NS), F32)
-    squares = centred * centred
-    plain[4:5, :] = squares[0:1] + squares[1:2] + squares[2:3] + SOFTENING_SQ
-    plain[5:8, :] = jnp.zeros((3, NS), F32)
-
-    def source_leaf(s, carry):
-        points = pl.ds(pl.multiple_of(s * LEAF, LEAF), LEAF)
-        high, middle, low = split3(plain[:, points] * weight[:, points])
-        stacked = jnp.concatenate([high, high, middle, middle, high, low], 0)
-        source_feat[s] = stacked.T.astype(BF16)
-        return carry
-
-    lax.fori_loop(0, CL, source_leaf, 0)
-
-    away = target_points[...] - 0.5
-    scaled[0:3, :] = away
-    squares = away * away
-    scaled[3:4, :] = squares[0:1] + squares[1:2] + squares[2:3]
-    scaled[4:5, :] = jnp.ones((1, NT), F32)
-    scaled[5:8, :] = jnp.zeros((3, NT), F32)
-
-    def target_leaf(t, carry):
-        points = pl.ds(pl.multiple_of(t * LEAF, LEAF), LEAF)
-        high, middle, low = split3(scaled[:, points])
-        stacked = jnp.concatenate([high, middle, high, middle, low, high], 0)
-        target_feat[t] = stacked.astype(BF16)
-        return carry
-
-    lax.fori_loop(0, RL, target_leaf, 0)
-
     def entry_step(step, carry):
         for u in range(ENTRY_UNROLL):
             k = step * ENTRY_UNROLL + u
@@ -223,21 +225,20 @@
         x_copy(dx, dz).wait_recv()
         go(pair_copy(dz, dx))
 
-    some_entries(0, 48)
+    some_entries(0, 64)
     from_z(1)
     from_z(3)
-    some_entries(48, 80)
+    some_entries(64, 96)
     from_z(2)
     for dx in (1, 3, 2):
         from_x(dx, 0)
-    some_entries(80, 144)
+    some_entries(96, 192)
     for dz in (1, 3):
         for dx in (1, 3, 2):
             from_x(dx, dz)
-    some_entries(144, 224)
+    some_entries(192, NEAR)
     for dx in (1, 3, 2):
         from_x(dx, 2)
-    some_entries(224, NEAR)
     own_copy.wait()
     for dz in range(4):
         for dx in range(4):
@@ -260,26 +261,35 @@
     sums[ZERO] = jnp.zeros((RHS, LEAF), F32)
     rank_lane = lax.broadcasted_iota(jnp.int32, (RHS, RANK), 1)
 
-    def far_step(step, carry):
-        blocks = []
+    def far_coefficients(step):
         for u in range(FAR_UNROLL):
             k = step * FAR_UNROLL + u
-            coefficients = lax.dot_general(
+            value = lax.dot_general(
                 grid[far_source[0, k]],
                 right[k],
                 (((1,), (1,)), ((), ())),
                 preferred_element_type=F32,
             )
-            coefficients = jnp.where(rank_lane < far_rank[0, k], coefficients, 0.0)
-            blocks.append(
-                jnp.dot(coefficients.astype(BF16), left[k], preferred_element_type=F32)
-            )
+            value = jnp.where(rank_lane < far_rank[0, k], value, 0.0)
+            coefficients[k] = value.astype(BF16)
+
+    def far_sums(step):
+        blocks = []
+        for u in range(FAR_UNROLL):
+            k = step * FAR_UNROLL + u
+            blocks.append(jnp.dot(coefficients[k], left[k], preferred_element_type=F32))
         for u in range(FAR_UNROLL):
             k = step * FAR_UNROLL + u
             sums[FAR_BASE + k] = blocks[u] + sums[far_prev[0, k]]
-        return carry
-
-    lax.fori_loop(0, FAR // FAR_UNROLL, far_step, 0)
+
+    def far_step(step, carry):
+        far_sums(step)
+        far_coefficients(step + 1)
+        return carry
+
+    far_coefficients(0)
+    lax.fori_loop(0, FAR // FAR_UNROLL - 1, far_step, 0)
+    far_sums(FAR // FAR_UNROLL - 1)
 
     for t in range(RL):
         sums[t] = sums[far_last[0, t]]
@@ -298,28 +308,31 @@
 
     lax.fori_loop(0, NEAR // NEAR_UNROLL, near_step, 0)
 
+    along = col // 2
+    side = lax.rem(col, 2)
+
     def pack_target(t, carry):
         points = pl.ds(pl.multiple_of(t * LEAF, LEAF), LEAF)
-        value = jnp.where(lane < target_fill[t], sums[near_last[0, t]], 0.0).astype(BF16)
-        for c in range(N_COL):
-            outgoing[c, :, points] = value[4 * c : 4 * c + 4]
+        value = jnp.where(lane < target_fill[t], sums[near_last[0, t]], 0.0)
+        for c in range(N_COL // 2):
+            first = value[8 * c : 8 * c + 4]
+            second = value[8 * c + 4 : 8 * c + 8]
+            kept[c, :, points] = jnp.where(side == 0, first, second)
+            outgoing[c, :, points] = jnp.where(side == 0, second, first).astype(BF16)
         return carry
 
     lax.fori_loop(0, RL, pack_target, 0)
 
-    along = col // 2
-    side = lax.rem(col, 2)
-
-    def owner(d, which):
-        return lax.rem(along + d, 8) * 2 + which
+    def owner(d):
+        return lax.rem(along + d, 8)
 
     def side_copy(d):
         return pltpu.make_async_remote_copy(
-            src_ref=outgoing.at[owner(d, 1 - side)],
+            src_ref=outgoing.at[owner(d)],
             dst_ref=from_side.at[d],
             send_sem=side_send.at[d],
             recv_sem=side_recv.at[d],
-            device_id=(row, owner(0, 1 - side)),
+            device_id=(row, along * 2 + 1 - side),
             device_id_type=MESH,
         )
 
@@ -329,7 +342,7 @@
             dst_ref=from_along.at[d - 1],
             send_sem=along_send.at[d - 1],
             recv_sem=along_recv.at[d - 1],
-            device_id=(row, owner(d, side)),
+            device_id=(row, owner(d) * 2 + side),
             device_id_type=MESH,
         )
 
@@ -338,7 +351,7 @@
         side_copy(d).start()
     for d in order:
         side_copy(d).wait_recv()
-        both = outgoing[owner(d, side)].astype(F32) + from_side[d].astype(F32)
+        both = kept[owner(d)] + from_side[d].astype(F32)
         merged[d] = both.astype(BF16)
         along_copy(d).start()
     side_copy(0).wait_recv()
@@ -347,7 +360,7 @@
 
     def add_up(step, carry):
         points = pl.ds(pl.multiple_of(step * 512, 512), 512)
-        total = outgoing[col, :, points].astype(F32) + from_side[0, :, points].astype(F32)
+        total = kept[along, :, points] + from_side[0, :, points].astype(F32)
         for d in order:
             total = total + from_along[d - 1, :, points].astype(F32)
         out[:, points] = total
@@ -437,7 +450,9 @@
             pltpu.VMEM((8, NS), F32),
             pltpu.VMEM((FAR, RANK, LEAF), BF16),
             pltpu.VMEM((FAR, RANK, LEAF), BF16),
-            pltpu.VMEM((N_COL, RHS // N_COL, NT), BF16),
+            pltpu.VMEM((FAR, RHS, RANK), BF16),
+            pltpu.VMEM((N_COL // 2, RHS // N_COL, NT), BF16),
+            pltpu.VMEM((N_COL // 2, RHS // N_COL, NT), F32),
             pltpu.VMEM((8, RHS // N_COL, NT), BF16),
             pltpu.VMEM((8, RHS // N_COL, NT), BF16),
             pltpu.VMEM((7, RHS // N_COL, NT), BF16),

time: 59.8 us -> 59 us (0.987)
  Pallas kernels: 57.4 us -> 56.7 us
    pallas_call x1, Pallas kernels: 56 us -> 55.3 us  [shards(): pl.pallas_call(kernel, name='block_low_rank', out_shape=jax.ShapeDtypeStr...]
where the time goes in v1:
time: 59 us; the launch traced here: 58.9 us
  Pallas kernels  56.7 us (96%)
  local copies, waits for them, and re-layouts  1.47 us (2%)
  between operations  0.66 us (1%)
    pallas_call x1, Pallas kernels, shards(): pl.pallas_call(kernel, name='block_low_rank', out_shape=jax.ShapeDtypeStr...  55.3 us
    unnamed x1, local copies, waits for them, and re-layouts  1.47 us
    pallas_call x1, Pallas kernels, shards(): pl.pallas_call(chain_kernel, name='chains', out_shape=[jax.ShapeDtypeStru...  1.43 us

profile of v1, /device:TPU:1, one launch (start us, length us, event | category | flops | bytes accessed | tf_op | source)
XLA Modules:
  0.0 58.9 jit_solution(266438113107437004)
XLA Ops:
  0.7 1.4 %chains.1 = (s32[1,256]{1,0:T(1,128)}, s32[1,128]{1,0:T(1,128)}, s32[1,128]{1,0:T(1,128)}, s32[1,128]{1,0:T(1,128)}) custom-call(s32[1,256]{1,0:T(1,128)} %near_target.3, s32[1,96]{1,0:T(1,128)} %far_target.1, s32[1,1]{1,0:T(1,128)S(6)} %copy.16.near_fill), custom_call_target="tpu_custom_call" | custom-call | tf_op jit(solution)/shard_map/chains/pallas_call | solution.py:423
  2.1 55.3 %block_low_rank.1 = f32[4,4096]{1,0:T(4,128)} custom-call(s32[1,256]{1,0:T(1,128)} %get-tuple-element.9.near_prev, s32[1,128]{1,0:T(1,128)} %get-tuple-element.10.near_last, s32[1,128]{1,0:T(1,128)} %get-tuple-element.11.far_prev, s32[1,128]{1,0:T(1,128)} %get-tuple-element.12.far_last, s32[1,256]{1,0:T(1,128)} %near_source.1, s32[1,256]{1,0:T(1,128)} %near_target.3, ...), custom_call_target="tpu_custom_call" | custom-call | tf_op jit(solution)/shard_map/block_low_rank/pallas_call | solution.py:435
  57.4 1.5 %copy.17 = f32[4,4096]{1,0:T(4,128)} copy(f32[4,4096]{1,0:T(4,128)} %block_low_rank.1) | data formatting | bytes 131072

commit v2 on v1

--- a/solution.py
+++ b/solution.py
@@ -29,6 +29,9 @@
 FAR_UNROLL = 16
 NEAR_UNROLL = 32
 LANES = 128
+LEAF_UNROLL = 8
+HALF = LEAF // 2
+NT_HALF = NT // 2
 F32 = jnp.float32
 BF16 = jnp.bfloat16
 
@@ -131,15 +134,6 @@
     plain[4:5, :] = squares[0:1] + squares[1:2] + squares[2:3] + SOFTENING_SQ
     plain[5:8, :] = jnp.zeros((3, NS), F32)
 
-    def source_leaf(s, carry):
-        points = pl.ds(pl.multiple_of(s * LEAF, LEAF), LEAF)
-        high, middle, low = split3(plain[:, points] * weight[:, points])
-        stacked = jnp.concatenate([high, high, middle, middle, high, low], 0)
-        source_feat[s] = stacked.T.astype(BF16)
-        return carry
-
-    lax.fori_loop(0, CL, source_leaf, 0)
-
     away = target_points[...] - 0.5
     scaled[0:3, :] = away
     squares = away * away
@@ -147,14 +141,16 @@
     scaled[4:5, :] = jnp.ones((1, NT), F32)
     scaled[5:8, :] = jnp.zeros((3, NT), F32)
 
-    def target_leaf(t, carry):
-        points = pl.ds(pl.multiple_of(t * LEAF, LEAF), LEAF)
-        high, middle, low = split3(scaled[:, points])
-        stacked = jnp.concatenate([high, middle, high, middle, low, high], 0)
-        target_feat[t] = stacked.astype(BF16)
-        return carry
-
-    lax.fori_loop(0, RL, target_leaf, 0)
+    def target_leaves(step, carry):
+        for u in range(LEAF_UNROLL):
+            t = step * LEAF_UNROLL + u
+            points = pl.ds(pl.multiple_of(t * LEAF, LEAF), LEAF)
+            high, middle, low = split3(scaled[:, points])
+            stacked = jnp.concatenate([high, middle, high, middle, low, high], 0)
+            target_feat[t] = stacked.astype(BF16)
+        return carry
+
+    lax.fori_loop(0, RL // LEAF_UNROLL, target_leaves, 0)
 
     pl.semaphore_wait(barrier, len(peers) + N_COL - 1)
 
@@ -201,6 +197,17 @@
         go(x_copy(dx, 0))
     go(pair_copy(0, 0))
 
+    def source_leaves(step, carry):
+        for u in range(LEAF_UNROLL):
+            s = step * LEAF_UNROLL + u
+            points = pl.ds(pl.multiple_of(s * LEAF, LEAF), LEAF)
+            high, middle, low = split3(plain[:, points] * weight[:, points])
+            stacked = jnp.concatenate([high, high, middle, middle, high, low], 0)
+            source_feat[s] = stacked.T.astype(BF16)
+        return carry
+
+    lax.fori_loop(0, CL // LEAF_UNROLL, source_leaves, 0)
+
     def entry_step(step, carry):
         for u in range(ENTRY_UNROLL):
             k = step * ENTRY_UNROLL + u
@@ -225,18 +232,18 @@
         x_copy(dx, dz).wait_recv()
         go(pair_copy(dz, dx))
 
-    some_entries(0, 64)
+    some_entries(0, 96)
     from_z(1)
     from_z(3)
-    some_entries(64, 96)
+    some_entries(96, 128)
     from_z(2)
     for dx in (1, 3, 2):
         from_x(dx, 0)
-    some_entries(96, 192)
+    some_entries(128, 224)
     for dz in (1, 3):
         for dx in (1, 3, 2):
             from_x(dx, dz)
-    some_entries(192, NEAR)
+    some_entries(224, NEAR)
     for dx in (1, 3, 2):
         from_x(dx, 2)
     own_copy.wait()
@@ -273,104 +280,133 @@
             value = jnp.where(rank_lane < far_rank[0, k], value, 0.0)
             coefficients[k] = value.astype(BF16)
 
-    def far_sums(step):
+    def far_sums(first, count, lanes):
         blocks = []
-        for u in range(FAR_UNROLL):
-            k = step * FAR_UNROLL + u
-            blocks.append(jnp.dot(coefficients[k], left[k], preferred_element_type=F32))
-        for u in range(FAR_UNROLL):
-            k = step * FAR_UNROLL + u
-            sums[FAR_BASE + k] = blocks[u] + sums[far_prev[0, k]]
-
-    def far_step(step, carry):
-        far_sums(step)
-        far_coefficients(step + 1)
-        return carry
-
-    far_coefficients(0)
-    lax.fori_loop(0, FAR // FAR_UNROLL - 1, far_step, 0)
-    far_sums(FAR // FAR_UNROLL - 1)
-
-    for t in range(RL):
-        sums[t] = sums[far_last[0, t]]
-
-    def near_step(step, carry):
-        blocks = []
-        for u in range(NEAR_UNROLL):
-            k = step * NEAR_UNROLL + u
+        for u in range(count):
+            k = first + u
             blocks.append(
-                jnp.dot(grid[near_source[0, k]], entries[k], preferred_element_type=F32)
+                jnp.dot(coefficients[k], left[k, :, lanes], preferred_element_type=F32)
             )
-        for u in range(NEAR_UNROLL):
-            k = step * NEAR_UNROLL + u
-            sums[RL + k] = blocks[u] + sums[near_prev[0, k]]
-        return carry
-
-    lax.fori_loop(0, NEAR // NEAR_UNROLL, near_step, 0)
+        for u in range(count):
+            k = first + u
+            sums[FAR_BASE + k, :, lanes] = blocks[u] + sums[far_prev[0, k], :, lanes]
+
+    def near_half(lanes):
+        for t in range(RL):
+            sums[t, :, lanes] = sums[far_last[0, t], :, lanes]
+
+        def near_step(step, carry):
+            blocks = []
+            for u in range(NEAR_UNROLL):
+                k = step * NEAR_UNROLL + u
+                blocks.append(
+                    jnp.dot(
+                        grid[near_source[0, k]],
+                        entries[k, :, lanes],
+                        preferred_element_type=F32,
+                    )
+                )
+            for u in range(NEAR_UNROLL):
+                k = step * NEAR_UNROLL + u
+                sums[RL + k, :, lanes] = blocks[u] + sums[near_prev[0, k], :, lanes]
+            return carry
+
+        lax.fori_loop(0, NEAR // NEAR_UNROLL, near_step, 0)
 
     along = col // 2
     side = lax.rem(col, 2)
-
-    def pack_target(t, carry):
-        points = pl.ds(pl.multiple_of(t * LEAF, LEAF), LEAF)
-        value = jnp.where(lane < target_fill[t], sums[near_last[0, t]], 0.0)
-        for c in range(N_COL // 2):
-            first = value[8 * c : 8 * c + 4]
-            second = value[8 * c + 4 : 8 * c + 8]
-            kept[c, :, points] = jnp.where(side == 0, first, second)
-            outgoing[c, :, points] = jnp.where(side == 0, second, first).astype(BF16)
-        return carry
-
-    lax.fori_loop(0, RL, pack_target, 0)
+    half_lane = lax.broadcasted_iota(jnp.int32, (RHS, HALF), 1)
+
+    def pack_half(half, lanes):
+        def pack_target(t, carry):
+            points = pl.ds(pl.multiple_of(t * HALF, HALF), HALF)
+            live = half_lane + half * HALF < target_fill[t]
+            value = jnp.where(live, sums[near_last[0, t], :, lanes], 0.0)
+            for c in range(N_COL // 2):
+                first = value[8 * c : 8 * c + 4]
+                second = value[8 * c + 4 : 8 * c + 8]
+                kept[half, c, :, points] = jnp.where(side == 0, first, second)
+                outgoing[half, c, :, points] = jnp.where(side == 0, second, first).astype(BF16)
+            return carry
+
+        lax.fori_loop(0, RL, pack_target, 0)
 
     def owner(d):
         return lax.rem(along + d, 8)
 
-    def side_copy(d):
+    def side_copy(half, d):
         return pltpu.make_async_remote_copy(
-            src_ref=outgoing.at[owner(d)],
-            dst_ref=from_side.at[d],
-            send_sem=side_send.at[d],
-            recv_sem=side_recv.at[d],
+            src_ref=outgoing.at[half, owner(d)],
+            dst_ref=from_side.at[half, d],
+            send_sem=side_send.at[half, d],
+            recv_sem=side_recv.at[half, d],
             device_id=(row, along * 2 + 1 - side),
             device_id_type=MESH,
         )
 
-    def along_copy(d):
+    def along_copy(half, d):
         return pltpu.make_async_remote_copy(
-            src_ref=merged.at[d],
-            dst_ref=from_along.at[d - 1],
-            send_sem=along_send.at[d - 1],
-            recv_sem=along_recv.at[d - 1],
+            src_ref=merged.at[half, d],
+            dst_ref=from_along.at[half, d - 1],
+            send_sem=along_send.at[half, d - 1],
+            recv_sem=along_recv.at[half, d - 1],
             device_id=(row, owner(d) * 2 + side),
             device_id_type=MESH,
         )
 
     order = (4, 3, 5, 2, 6, 1, 7)
+
+    def merge_half(half):
+        for d in order:
+            side_copy(half, d).wait_recv()
+            both = kept[half, owner(d)] + from_side[half, d].astype(F32)
+            merged[half, d] = both.astype(BF16)
+            along_copy(half, d).start()
+
+    def far_step(step, carry):
+        far_sums(step * FAR_UNROLL, FAR_UNROLL, pl.ds(0, HALF))
+        far_coefficients(step + 1)
+        return carry
+
+    far_coefficients(0)
+    lax.fori_loop(0, FAR // FAR_UNROLL - 1, far_step, 0)
+    far_sums(FAR - FAR_UNROLL, FAR_UNROLL, pl.ds(0, HALF))
+    near_half(pl.ds(0, HALF))
+    pack_half(0, pl.ds(0, HALF))
     for d in order + (0,):
-        side_copy(d).start()
-    for d in order:
-        side_copy(d).wait_recv()
-        both = kept[owner(d)] + from_side[d].astype(F32)
-        merged[d] = both.astype(BF16)
-        along_copy(d).start()
-    side_copy(0).wait_recv()
-    for d in order:
-        along_copy(d).wait_recv()
-
-    def add_up(step, carry):
-        points = pl.ds(pl.multiple_of(step * 512, 512), 512)
-        total = kept[along, :, points] + from_side[0, :, points].astype(F32)
+        side_copy(0, d).start()
+
+    def far_second(step, carry):
+        far_sums(step * NEAR_UNROLL, NEAR_UNROLL, pl.ds(HALF, HALF))
+        return carry
+
+    lax.fori_loop(0, FAR // NEAR_UNROLL, far_second, 0)
+    near_half(pl.ds(HALF, HALF))
+    pack_half(1, pl.ds(HALF, HALF))
+    for d in order + (0,):
+        side_copy(1, d).start()
+    merge_half(0)
+    merge_half(1)
+    for half in range(2):
+        side_copy(half, 0).wait_recv()
         for d in order:
-            total = total + from_along[d - 1, :, points].astype(F32)
-        out[:, points] = total
-        return carry
-
-    lax.fori_loop(0, NT // 512, add_up, 0)
-    for d in order:
-        along_copy(d).wait_send()
-        side_copy(d).wait_send()
-    side_copy(0).wait_send()
+            along_copy(half, d).wait_recv()
+
+    def add_up(t, carry):
+        for half in range(2):
+            points = pl.ds(pl.multiple_of(t * HALF, HALF), HALF)
+            total = kept[half, along, :, points] + from_side[half, 0, :, points].astype(F32)
+            for d in order:
+                total = total + from_along[half, d - 1, :, points].astype(F32)
+            out[:, pl.ds(pl.multiple_of(t * LEAF + half * HALF, HALF), HALF)] = total
+        return carry
+
+    lax.fori_loop(0, RL, add_up, 0)
+    for half in range(2):
+        for d in order:
+            along_copy(half, d).wait_send()
+            side_copy(half, d).wait_send()
+        side_copy(half, 0).wait_send()
 
 
 def chain_kernel(near_target, far_target, near_fill, near_prev, near_last, far_prev, far_last):
@@ -451,11 +487,11 @@
             pltpu.VMEM((FAR, RANK, LEAF), BF16),
             pltpu.VMEM((FAR, RANK, LEAF), BF16),
             pltpu.VMEM((FAR, RHS, RANK), BF16),
-            pltpu.VMEM((N_COL // 2, RHS // N_COL, NT), BF16),
-            pltpu.VMEM((N_COL // 2, RHS // N_COL, NT), F32),
-            pltpu.VMEM((8, RHS // N_COL, NT), BF16),
-            pltpu.VMEM((8, RHS // N_COL, NT), BF16),
-            pltpu.VMEM((7, RHS // N_COL, NT), BF16),
+            pltpu.VMEM((2, 8, RHS // N_COL, NT_HALF), BF16),
+            pltpu.VMEM((2, 8, RHS // N_COL, NT_HALF), F32),
+            pltpu.VMEM((2, 8, RHS // N_COL, NT_HALF), BF16),
+            pltpu.VMEM((2, 8, RHS // N_COL, NT_HALF), BF16),
+            pltpu.VMEM((2, 7, RHS // N_COL, NT_HALF), BF16),
             dma(()),
             dma((2,)),
             dma((3,)),
@@ -464,10 +500,10 @@
             dma((3, 4)),
             dma((4, 4)),
             dma((4, 4)),
-            dma((8,)),
-            dma((8,)),
-            dma((7,)),
-            dma((7,)),
+            dma((2, 8)),
+            dma((2, 8)),
+            dma((2, 7)),
+            dma((2, 7)),
         ],
         compiler_params=pltpu.CompilerParams(
             collective_id=0, has_side_effects=True, vmem_limit_bytes=64 * 1024 * 1024 - 65536

time: 59 us -> 55.5 us (0.941)
  Pallas kernels: 56.7 us -> 53.1 us
    pallas_call x1, Pallas kernels: 55.3 us -> 51.7 us  [shards(): pl.pallas_call(kernel, name='block_low_rank', out_shape=jax.ShapeDtypeStr...]
where the time goes in v2:
time: 55.5 us; the launch traced here: 55.2 us
  Pallas kernels  53.1 us (96%)
  local copies, waits for them, and re-layouts  1.47 us (3%)
  between operations  0.66 us (1%)
    pallas_call x1, Pallas kernels, shards(): pl.pallas_call(kernel, name='block_low_rank', out_shape=jax.ShapeDtypeStr...  51.7 us
    unnamed x1, local copies, waits for them, and re-layouts  1.47 us
    pallas_call x1, Pallas kernels, shards(): pl.pallas_call(chain_kernel, name='chains', out_shape=[jax.ShapeDtypeStru...  1.43 us

profile of v2, /device:TPU:1, one launch (start us, length us, event | category | flops | bytes accessed | tf_op | source)
XLA Modules:
  0.0 55.2 jit_solution(14344804880520971596)
XLA Ops:
  0.7 1.4 %chains.1 = (s32[1,256]{1,0:T(1,128)}, s32[1,128]{1,0:T(1,128)}, s32[1,128]{1,0:T(1,128)}, s32[1,128]{1,0:T(1,128)}) custom-call(s32[1,256]{1,0:T(1,128)} %near_target.3, s32[1,96]{1,0:T(1,128)} %far_target.1, s32[1,1]{1,0:T(1,128)S(6)} %copy.16.near_fill), custom_call_target="tpu_custom_call" | custom-call | tf_op jit(solution)/shard_map/chains/pallas_call | solution.py:459
  2.1 51.7 %block_low_rank.1 = f32[4,4096]{1,0:T(4,128)} custom-call(s32[1,256]{1,0:T(1,128)} %get-tuple-element.9.near_prev, s32[1,128]{1,0:T(1,128)} %get-tuple-element.10.near_last, s32[1,128]{1,0:T(1,128)} %get-tuple-element.11.far_prev, s32[1,128]{1,0:T(1,128)} %get-tuple-element.12.far_last, s32[1,256]{1,0:T(1,128)} %near_source.1, s32[1,256]{1,0:T(1,128)} %near_target.3, ...), custom_call_target="tpu_custom_call" | custom-call | tf_op jit(solution)/shard_map/block_low_rank/pallas_call | solution.py:471
  53.8 1.5 %copy.17 = f32[4,4096]{1,0:T(4,128)} copy(f32[4,4096]{1,0:T(4,128)} %block_low_rank.1) | data formatting | bytes 131072

commit v3 on v2

--- a/solution.py
+++ b/solution.py
@@ -31,6 +31,7 @@
 LANES = 128
 LEAF_UNROLL = 8
 HALF = LEAF // 2
+NEAR_STEPS = NEAR // NEAR_UNROLL
 NT_HALF = NT // 2
 F32 = jnp.float32
 BF16 = jnp.bfloat16
@@ -44,21 +45,37 @@
     return high, middle, low
 
 
+def chains(target, count, place, empty):
+    across = jnp.broadcast_to(target, (count, count))
+    down = across.T
+    at_down = lax.broadcasted_iota(jnp.int32, (count, count), 0)
+    at_across = lax.broadcasted_iota(jnp.int32, (count, count), 1)
+    hit = (across == down) & (at_down < at_across)
+    prev = jnp.max(jnp.where(hit, at_down + place, -1), axis=0, keepdims=True)
+    return jnp.maximum(prev, empty), down
+
+
+def latest(down, count, place, live, empty):
+    slot = lax.broadcasted_iota(jnp.int32, (count, LANES), 0)
+    leaf = lax.broadcasted_iota(jnp.int32, (count, LANES), 1)
+    hit = (down[:, :LANES] == leaf) & (slot < live)
+    last = jnp.max(jnp.where(hit, slot + place, -1), axis=0, keepdims=True)
+    return jnp.maximum(last, empty)
+
+
 def kernel(
-    near_prev,
-    near_last,
-    far_prev,
-    far_last,
-    near_source,
-    near_target,
-    far_source,
-    far_rank,
-    source_fill,
-    target_fill,
-    source_points,
-    source_areas,
-    target_points,
-    charges,
+    near_target_hbm,
+    far_target_hbm,
+    near_fill,
+    near_source_hbm,
+    far_source_hbm,
+    far_rank_hbm,
+    source_fill_hbm,
+    target_fill_hbm,
+    source_points_hbm,
+    source_areas_hbm,
+    target_points_hbm,
+    charges_hbm,
     left_hbm,
     right_hbm,
     out,
@@ -79,8 +96,26 @@
     from_side,
     merged,
     from_along,
-    own_sem,
-    basis_sem,
+    source_points,
+    source_areas,
+    target_points,
+    near_across,
+    far_across,
+    near_prev_row,
+    near_last_row,
+    far_prev_row,
+    far_last_row,
+    near_target,
+    near_source,
+    far_source,
+    far_rank,
+    source_fill,
+    target_fill,
+    near_prev,
+    near_last,
+    far_prev,
+    far_last,
+    local_sem,
     z_send,
     z_recv,
     x_send,
@@ -107,13 +142,6 @@
     def ahead(a, d):
         return lax.rem(a + d, 4)
 
-    own_copy = pltpu.make_async_copy(charges, grid_raw.at[row], own_sem)
-    own_copy.start()
-    left_copy = pltpu.make_async_copy(left_hbm.at[0], left, basis_sem.at[0])
-    right_copy = pltpu.make_async_copy(right_hbm.at[0], right, basis_sem.at[1])
-    left_copy.start()
-    right_copy.start()
-
     barrier = pltpu.get_barrier_semaphore()
     partner = row_of(z, x, 1 - core)
     peers = [partner]
@@ -125,6 +153,49 @@
         pl.semaphore_signal(
             barrier, inc=1, device_id=(row, lax.rem(col + d, N_COL)), device_id_type=MESH
         )
+    local = []
+
+    def fetch(source, target):
+        copy = pltpu.make_async_copy(source, target, local_sem.at[len(local)])
+        copy.start()
+        local.append(copy)
+        return copy
+
+    own_copy = fetch(charges_hbm, grid_raw.at[row])
+    charges = grid_raw.at[row]
+    point_copies = [
+        fetch(target_points_hbm, target_points),
+        fetch(source_points_hbm, source_points),
+        fetch(source_areas_hbm, source_areas),
+    ]
+    chain_copies = [
+        fetch(near_target_hbm, near_across),
+        fetch(far_target_hbm, far_across),
+    ]
+    index_copies = [
+        fetch(near_source_hbm, near_source),
+        fetch(near_target_hbm, near_target),
+        fetch(far_source_hbm, far_source),
+        fetch(far_rank_hbm, far_rank),
+        fetch(source_fill_hbm, source_fill),
+        fetch(target_fill_hbm, target_fill),
+    ]
+    left_copy = fetch(left_hbm.at[0], left)
+    right_copy = fetch(right_hbm.at[0], right)
+    for copy in chain_copies + point_copies:
+        copy.wait()
+
+    prev, down = chains(near_across[...], NEAR, RL, near_across[...])
+    near_prev_row[...] = prev
+    leaf_lane = lax.broadcasted_iota(jnp.int32, (1, LANES), 1)
+    near_last_row[...] = latest(down, NEAR, RL, near_fill[0, 0], jnp.minimum(leaf_lane, RL - 1))
+    padding = jnp.full((1, LANES - FAR), RL, jnp.int32)
+    prev, down = chains(
+        jnp.concatenate([far_across[...], padding], 1), LANES, FAR_BASE, ZERO
+    )
+    far_prev_row[...] = prev
+    far_last_row[...] = latest(down, LANES, FAR_BASE, FAR, ZERO)
+
     centred = source_points[...] - 0.5
     area = source_areas[...].reshape(1, NS) * INV_FOUR_PI
     weight[...] = 1.0 / (area * area)
@@ -152,6 +223,7 @@
 
     lax.fori_loop(0, RL // LEAF_UNROLL, target_leaves, 0)
 
+    own_copy.wait()
     pl.semaphore_wait(barrier, len(peers) + N_COL - 1)
 
     def send(source, slot, peer, send_sem, recv_sem):
@@ -207,6 +279,15 @@
         return carry
 
     lax.fori_loop(0, CL // LEAF_UNROLL, source_leaves, 0)
+
+    table_copies = [
+        fetch(near_prev_row, near_prev),
+        fetch(near_last_row, near_last),
+        fetch(far_prev_row, far_prev),
+        fetch(far_last_row, far_last),
+    ]
+    for copy in index_copies:
+        copy.wait()
 
     def entry_step(step, carry):
         for u in range(ENTRY_UNROLL):
@@ -246,13 +327,9 @@
     some_entries(224, NEAR)
     for dx in (1, 3, 2):
         from_x(dx, 2)
-    own_copy.wait()
     for dz in range(4):
         for dx in range(4):
             pair_copy(dz, dx).wait_recv()
-    for copy in started:
-        copy.wait_send()
-
     lane = lax.broadcasted_iota(jnp.int32, (RHS, LEAF), 1)
 
     def charge_leaf(s, carry):
@@ -265,6 +342,8 @@
 
     left_copy.wait()
     right_copy.wait()
+    for copy in table_copies:
+        copy.wait()
     sums[ZERO] = jnp.zeros((RHS, LEAF), F32)
     rank_lane = lax.broadcasted_iota(jnp.int32, (RHS, RANK), 1)
 
@@ -291,10 +370,11 @@
             k = first + u
             sums[FAR_BASE + k, :, lanes] = blocks[u] + sums[far_prev[0, k], :, lanes]
 
-    def near_half(lanes):
+    def near_start(lanes):
         for t in range(RL):
             sums[t, :, lanes] = sums[far_last[0, t], :, lanes]
 
+    def near_part(lanes, first, last):
         def near_step(step, carry):
             blocks = []
             for u in range(NEAR_UNROLL):
@@ -311,7 +391,7 @@
                 sums[RL + k, :, lanes] = blocks[u] + sums[near_prev[0, k], :, lanes]
             return carry
 
-        lax.fori_loop(0, NEAR // NEAR_UNROLL, near_step, 0)
+        lax.fori_loop(first, last, near_step, 0)
 
     along = col // 2
     side = lax.rem(col, 2)
@@ -356,8 +436,8 @@
 
     order = (4, 3, 5, 2, 6, 1, 7)
 
-    def merge_half(half):
-        for d in order:
+    def merge_half(half, some):
+        for d in some:
             side_copy(half, d).wait_recv()
             both = kept[half, owner(d)] + from_side[half, d].astype(F32)
             merged[half, d] = both.astype(BF16)
@@ -371,7 +451,8 @@
     far_coefficients(0)
     lax.fori_loop(0, FAR // FAR_UNROLL - 1, far_step, 0)
     far_sums(FAR - FAR_UNROLL, FAR_UNROLL, pl.ds(0, HALF))
-    near_half(pl.ds(0, HALF))
+    near_start(pl.ds(0, HALF))
+    near_part(pl.ds(0, HALF), 0, NEAR_STEPS)
     pack_half(0, pl.ds(0, HALF))
     for d in order + (0,):
         side_copy(0, d).start()
@@ -381,12 +462,19 @@
         return carry
 
     lax.fori_loop(0, FAR // NEAR_UNROLL, far_second, 0)
-    near_half(pl.ds(HALF, HALF))
+    near_start(pl.ds(HALF, HALF))
+    near_part(pl.ds(HALF, HALF), 0, NEAR_STEPS - 3)
+    merge_half(0, order[0:1])
+    near_part(pl.ds(HALF, HALF), NEAR_STEPS - 3, NEAR_STEPS - 2)
+    merge_half(0, order[1:3])
+    near_part(pl.ds(HALF, HALF), NEAR_STEPS - 2, NEAR_STEPS - 1)
+    merge_half(0, order[3:5])
+    near_part(pl.ds(HALF, HALF), NEAR_STEPS - 1, NEAR_STEPS)
     pack_half(1, pl.ds(HALF, HALF))
     for d in order + (0,):
         side_copy(1, d).start()
-    merge_half(0)
-    merge_half(1)
+    merge_half(0, order[5:7])
+    merge_half(1, order)
     for half in range(2):
         side_copy(half, 0).wait_recv()
         for d in order:
@@ -407,33 +495,8 @@
             along_copy(half, d).wait_send()
             side_copy(half, d).wait_send()
         side_copy(half, 0).wait_send()
-
-
-def chain_kernel(near_target, far_target, near_fill, near_prev, near_last, far_prev, far_last):
-    def chains(target, count, place, empty):
-        across = jnp.broadcast_to(target, (count, count))
-        down = across.T
-        at_down = lax.broadcasted_iota(jnp.int32, (count, count), 0)
-        at_across = lax.broadcasted_iota(jnp.int32, (count, count), 1)
-        hit = (across == down) & (at_down < at_across)
-        prev = jnp.max(jnp.where(hit, at_down + place, -1), axis=0, keepdims=True)
-        return jnp.maximum(prev, empty), down
-
-    def latest(down, count, place, live, empty):
-        slot = lax.broadcasted_iota(jnp.int32, (count, LANES), 0)
-        leaf = lax.broadcasted_iota(jnp.int32, (count, LANES), 1)
-        hit = (down[:, :LANES] == leaf) & (slot < live)
-        last = jnp.max(jnp.where(hit, slot + place, -1), axis=0, keepdims=True)
-        return jnp.maximum(last, empty)
-
-    leaf = lax.broadcasted_iota(jnp.int32, (1, LANES), 1)
-    prev, down = chains(near_target[...], NEAR, RL, near_target[...])
-    near_prev[...] = prev
-    near_last[...] = latest(down, NEAR, RL, near_fill[0, 0], jnp.minimum(leaf, RL - 1))
-    far = jnp.concatenate([far_target[...], jnp.full((1, LANES - FAR), RL, jnp.int32)], 1)
-    prev, down = chains(far, LANES, FAR_BASE, ZERO)
-    far_prev[...] = prev
-    far_last[...] = latest(down, LANES, FAR_BASE, FAR, ZERO)
+    for copy in started:
+        copy.wait_send()
 
 
 def shards(
@@ -452,27 +515,14 @@
     left_basis,
     right_basis,
 ):
-    smem = pl.BlockSpec(memory_space=pltpu.SMEM)
     vmem = pl.BlockSpec(memory_space=pltpu.VMEM)
     hbm = pl.BlockSpec(memory_space=pl.ANY)
     dma = pltpu.SemaphoreType.DMA
-    chains = pl.pallas_call(
-        chain_kernel,
-        name="chains",
-        out_shape=[
-            jax.ShapeDtypeStruct((1, NEAR), jnp.int32),
-            jax.ShapeDtypeStruct((1, LANES), jnp.int32),
-            jax.ShapeDtypeStruct((1, LANES), jnp.int32),
-            jax.ShapeDtypeStruct((1, LANES), jnp.int32),
-        ],
-        in_specs=[vmem, vmem, smem],
-        out_specs=[vmem] * 4,
-    )(near_target, far_target, near_fill)
     return pl.pallas_call(
         kernel,
         name="block_low_rank",
         out_shape=jax.ShapeDtypeStruct((RHS // N_COL, NT), F32),
-        in_specs=[smem] * 10 + [vmem] * 4 + [hbm] * 2,
+        in_specs=[hbm] * 2 + [pl.BlockSpec(memory_space=pltpu.SMEM)] + [hbm] * 11,
         out_specs=vmem,
         scratch_shapes=[
             pltpu.VMEM((N_ROW, RHS // N_ROW, NS), BF16),
@@ -492,8 +542,26 @@
             pltpu.VMEM((2, 8, RHS // N_COL, NT_HALF), BF16),
             pltpu.VMEM((2, 8, RHS // N_COL, NT_HALF), BF16),
             pltpu.VMEM((2, 7, RHS // N_COL, NT_HALF), BF16),
-            dma(()),
-            dma((2,)),
+            pltpu.VMEM((3, NS), F32),
+            pltpu.VMEM((NS,), F32),
+            pltpu.VMEM((3, NT), F32),
+            pltpu.VMEM((1, NEAR), jnp.int32),
+            pltpu.VMEM((1, FAR), jnp.int32),
+            pltpu.VMEM((1, NEAR), jnp.int32),
+            pltpu.VMEM((1, LANES), jnp.int32),
+            pltpu.VMEM((1, LANES), jnp.int32),
+            pltpu.VMEM((1, LANES), jnp.int32),
+            pltpu.SMEM((1, NEAR), jnp.int32),
+            pltpu.SMEM((1, NEAR), jnp.int32),
+            pltpu.SMEM((1, FAR), jnp.int32),
+            pltpu.SMEM((1, FAR), jnp.int32),
+            pltpu.SMEM((CL,), jnp.int32),
+            pltpu.SMEM((RL,), jnp.int32),
+            pltpu.SMEM((1, NEAR), jnp.int32),
+            pltpu.SMEM((1, LANES), jnp.int32),
+            pltpu.SMEM((1, LANES), jnp.int32),
+            pltpu.SMEM((1, LANES), jnp.int32),
+            dma((18,)),
             dma((3,)),
             dma((3,)),
             dma((3, 4)),
@@ -509,9 +577,10 @@
             collective_id=0, has_side_effects=True, vmem_limit_bytes=64 * 1024 * 1024 - 65536
         ),
     )(
-        *chains,
+        near_target,
+        far_target,
+        near_fill,
         near_source,
-        near_target,
         far_source,
         far_rank,
         source_fill,

time: 55.5 us -> 52.1 us (0.939)
  Pallas kernels: 53.1 us -> 49.8 us
    pallas_call x1, Pallas kernels: 51.7 us -> 49.8 us  [shards(): pl.pallas_call(kernel, name='block_low_rank', out_shape=jax.ShapeDtypeStr...]
    pallas_call x1 -> x0, Pallas kernels: 1.43 us -> none  [shards(): pl.pallas_call(chain_kernel, name='chains', out_shape=[jax.ShapeDtypeStru...]
where the time goes in v3:
time: 52.1 us; the launch traced here: 51.9 us
  Pallas kernels  49.8 us (96%)
  local copies, waits for them, and re-layouts  1.47 us (3%)
  between operations  0.66 us (1%)
    pallas_call x1, Pallas kernels, shards(): pl.pallas_call(kernel, name='block_low_rank', out_shape=jax.ShapeDtypeStr...  49.8 us
    unnamed x1, local copies, waits for them, and re-layouts  1.47 us

profile of v3, /device:TPU:1, one launch (start us, length us, event | category | flops | bytes accessed | tf_op | source)
XLA Modules:
  0.0 51.9 jit_solution(3106961783922884005)
XLA Ops:
  0.7 49.8 %block_low_rank.1 = f32[4,4096]{1,0:T(4,128)} custom-call(s32[1,256]{1,0:T(1,128)} %near_target_hbm.1, s32[1,96]{1,0:T(1,128)} %far_target_hbm.1, s32[1,1]{1,0:T(1,128)S(6)} %copy.16.near_fill, s32[1,256]{1,0:T(1,128)} %near_source_hbm.1, s32[1,96]{1,0:T(1,128)} %far_source_hbm.1, s32[1,96]{1,0:T(1,128)} %far_rank_hbm.1, s32[32]{0:T(128)} %source_fill_hbm.1, ...), custom_call_target="tpu_custom_call" | custom-call | tf_op jit(solution)/shard_map/block_low_rank/pallas_call | solution.py:521
  50.5 1.5 %copy.17 = f32[4,4096]{1,0:T(4,128)} copy(f32[4,4096]{1,0:T(4,128)} %block_low_rank.1) | data formatting | bytes 131072

commit v4 on v3

--- a/solution.py
+++ b/solution.py
@@ -182,9 +182,84 @@
     ]
     left_copy = fetch(left_hbm.at[0], left)
     right_copy = fetch(right_hbm.at[0], right)
-    for copy in chain_copies + point_copies:
+    for copy in point_copies:
         copy.wait()
 
+    centred = source_points[...] - 0.5
+    area = source_areas[...].reshape(1, NS) * INV_FOUR_PI
+    weight[...] = 1.0 / (area * area)
+    plain[0:3, :] = centred * -2.0
+    plain[3:4, :] = jnp.ones((1, NS), F32)
+    squares = centred * centred
+    plain[4:5, :] = squares[0:1] + squares[1:2] + squares[2:3] + SOFTENING_SQ
+    plain[5:8, :] = jnp.zeros((3, NS), F32)
+
+    away = target_points[...] - 0.5
+    scaled[0:3, :] = away
+    squares = away * away
+    scaled[3:4, :] = squares[0:1] + squares[1:2] + squares[2:3]
+    scaled[4:5, :] = jnp.ones((1, NT), F32)
+    scaled[5:8, :] = jnp.zeros((3, NT), F32)
+
+    def target_leaves(step, carry):
+        for u in range(LEAF_UNROLL):
+            t = step * LEAF_UNROLL + u
+            points = pl.ds(pl.multiple_of(t * LEAF, LEAF), LEAF)
+            high, middle, low = split3(scaled[:, points])
+            stacked = jnp.concatenate([high, middle, high, middle, low, high], 0)
+            target_feat[t] = stacked.astype(BF16)
+        return carry
+
+    lax.fori_loop(0, RL // LEAF_UNROLL, target_leaves, 0)
+
+    own_copy.wait()
+    pl.semaphore_wait(barrier, len(peers) + N_COL - 1)
+
+    def send(source, slot, peer, send_sem, recv_sem):
+        return pltpu.make_async_remote_copy(
+            src_ref=source,
+            dst_ref=grid_raw.at[slot],
+            send_sem=send_sem,
+            recv_sem=recv_sem,
+            device_id=(peer, col),
+            device_id_type=MESH,
+        )
+
+    def z_copy(dz):
+        return send(
+            charges, row, row_of(ahead(z, dz), x, core), z_send.at[dz - 1], z_recv.at[dz - 1]
+        )
+
+    def x_copy(dx, dz):
+        slot = row_of(back(z, dz), x, core)
+        source = charges if dz == 0 else grid_raw.at[slot]
+        return send(
+            source,
+            slot,
+            row_of(z, ahead(x, dx), core),
+            x_send.at[dx - 1, dz],
+            x_recv.at[dx - 1, dz],
+        )
+
+    def pair_copy(dz, dx):
+        slot = row_of(back(z, dz), back(x, dx), core)
+        source = charges if dz == 0 and dx == 0 else grid_raw.at[slot]
+        return send(source, slot, partner, pair_send.at[dz, dx], pair_recv.at[dz, dx])
+
+    started = []
+
+    def go(copy):
+        copy.start()
+        started.append(copy)
+
+    for dz in (2, 1, 3):
+        go(z_copy(dz))
+    for dx in (2, 1, 3):
+        go(x_copy(dx, 0))
+    go(pair_copy(0, 0))
+
+    for copy in chain_copies:
+        copy.wait()
     prev, down = chains(near_across[...], NEAR, RL, near_across[...])
     near_prev_row[...] = prev
     leaf_lane = lax.broadcasted_iota(jnp.int32, (1, LANES), 1)
@@ -195,79 +270,6 @@
     )
     far_prev_row[...] = prev
     far_last_row[...] = latest(down, LANES, FAR_BASE, FAR, ZERO)
-
-    centred = source_points[...] - 0.5
-    area = source_areas[...].reshape(1, NS) * INV_FOUR_PI
-    weight[...] = 1.0 / (area * area)
-    plain[0:3, :] = centred * -2.0
-    plain[3:4, :] = jnp.ones((1, NS), F32)
-    squares = centred * centred
-    plain[4:5, :] = squares[0:1] + squares[1:2] + squares[2:3] + SOFTENING_SQ
-    plain[5:8, :] = jnp.zeros((3, NS), F32)
-
-    away = target_points[...] - 0.5
-    scaled[0:3, :] = away
-    squares = away * away
-    scaled[3:4, :] = squares[0:1] + squares[1:2] + squares[2:3]
-    scaled[4:5, :] = jnp.ones((1, NT), F32)
-    scaled[5:8, :] = jnp.zeros((3, NT), F32)
-
-    def target_leaves(step, carry):
-        for u in range(LEAF_UNROLL):
-            t = step * LEAF_UNROLL + u
-            points = pl.ds(pl.multiple_of(t * LEAF, LEAF), LEAF)
-            high, middle, low = split3(scaled[:, points])
-            stacked = jnp.concatenate([high, middle, high, middle, low, high], 0)
-            target_feat[t] = stacked.astype(BF16)
-        return carry
-
-    lax.fori_loop(0, RL // LEAF_UNROLL, target_leaves, 0)
-
-    own_copy.wait()
-    pl.semaphore_wait(barrier, len(peers) + N_COL - 1)
-
-    def send(source, slot, peer, send_sem, recv_sem):
-        return pltpu.make_async_remote_copy(
-            src_ref=source,
-            dst_ref=grid_raw.at[slot],
-            send_sem=send_sem,
-            recv_sem=recv_sem,
-            device_id=(peer, col),
-            device_id_type=MESH,
-        )
-
-    def z_copy(dz):
-        return send(
-            charges, row, row_of(ahead(z, dz), x, core), z_send.at[dz - 1], z_recv.at[dz - 1]
-        )
-
-    def x_copy(dx, dz):
-        slot = row_of(back(z, dz), x, core)
-        source = charges if dz == 0 else grid_raw.at[slot]
-        return send(
-            source,
-            slot,
-            row_of(z, ahead(x, dx), core),
-            x_send.at[dx - 1, dz],
-            x_recv.at[dx - 1, dz],
-        )
-
-    def pair_copy(dz, dx):
-        slot = row_of(back(z, dz), back(x, dx), core)
-        source = charges if dz == 0 and dx == 0 else grid_raw.at[slot]
-        return send(source, slot, partner, pair_send.at[dz, dx], pair_recv.at[dz, dx])
-
-    started = []
-
-    def go(copy):
-        copy.start()
-        started.append(copy)
-
-    for dz in (2, 1, 3):
-        go(z_copy(dz))
-    for dx in (2, 1, 3):
-        go(x_copy(dx, 0))
-    go(pair_copy(0, 0))
 
     def source_leaves(step, carry):
         for u in range(LEAF_UNROLL):
@@ -332,13 +334,15 @@
             pair_copy(dz, dx).wait_recv()
     lane = lax.broadcasted_iota(jnp.int32, (RHS, LEAF), 1)
 
-    def charge_leaf(s, carry):
-        points = pl.ds(pl.multiple_of(s * LEAF, LEAF), LEAF)
-        block = grid_raw[:, :, points].reshape(RHS, LEAF)
-        grid[s] = jnp.where(lane < source_fill[s], block.astype(F32), 0.0).astype(BF16)
+    def charge_leaves(step, carry):
+        for u in range(LEAF_UNROLL):
+            s = step * LEAF_UNROLL + u
+            points = pl.ds(pl.multiple_of(s * LEAF, LEAF), LEAF)
+            block = grid_raw[:, :, points].reshape(RHS, LEAF).astype(F32)
+            grid[s] = jnp.where(lane < source_fill[s], block, 0.0).astype(BF16)
         return carry
 
-    lax.fori_loop(0, CL, charge_leaf, 0)
+    lax.fori_loop(0, CL // LEAF_UNROLL, charge_leaves, 0)
 
     left_copy.wait()
     right_copy.wait()

time: 52.1 us -> 51.9 us (level)
  no operation moved by 1% of the time
where the time goes in v4:
time: 51.9 us; the launch traced here: 51.7 us
  Pallas kernels  49.6 us (96%)
  local copies, waits for them, and re-layouts  1.47 us (3%)
  between operations  0.66 us (1%)
    pallas_call x1, Pallas kernels, shards(): pl.pallas_call(kernel, name='block_low_rank', out_shape=jax.ShapeDtypeStr...  49.6 us
    unnamed x1, local copies, waits for them, and re-layouts  1.47 us

profile of v4, /device:TPU:1, one launch (start us, length us, event | category | flops | bytes accessed | tf_op | source)
XLA Modules:
  0.0 51.7 jit_solution(6542224317272060764)
XLA Ops:
  0.7 49.6 %block_low_rank.1 = f32[4,4096]{1,0:T(4,128)} custom-call(s32[1,256]{1,0:T(1,128)} %near_target_hbm.1, s32[1,96]{1,0:T(1,128)} %far_target_hbm.1, s32[1,1]{1,0:T(1,128)S(6)} %copy.16.near_fill, s32[1,256]{1,0:T(1,128)} %near_source_hbm.1, s32[1,96]{1,0:T(1,128)} %far_source_hbm.1, s32[1,96]{1,0:T(1,128)} %far_rank_hbm.1, s32[32]{0:T(128)} %source_fill_hbm.1, ...), custom_call_target="tpu_custom_call" | custom-call | tf_op jit(solution)/shard_map/block_low_rank/pallas_call | solution.py:525
  50.3 1.5 %copy.17 = f32[4,4096]{1,0:T(4,128)} copy(f32[4,4096]{1,0:T(4,128)} %block_low_rank.1) | data formatting | bytes 131072
